TPU v7x, 32 devices: a whole 2x2x4 slice. The times are simulated.
32 devices in a mesh: grp: 2 (over y), slab: 4 (over z), ang: 4 (over x, core).
Axes of the slice: x: 2, y: 2, z: 4, core: 2. Of those that a mesh axis runs over, the one named last changes fastest.
Arguments:
- volume: bfloat16 [16, 256, 1024], P(('grp', 'slab')), parts along dimension 0, may hold values from -6 to 6
- ray_weights: bfloat16 [8, 1024, 1024], P('ang'), may hold values from -0.0625 to 0.0625
- row_offsets: int32 [8, 8], P('ang'), may hold values from 0 to 8
- measured: float32 [16, 256, 1024], P(('grp', 'ang'), 'slab'), parts along dimension 0, may hold values from -6 to 6
- shifts: float32 [16], P(('grp', 'ang')), parts along dimension 0, may hold values from -4 to 4
Outputs:
- updated_volume: bfloat16 [16, 256, 1024], P(('grp', 'slab')), parts along dimension 0
- last_residual: float32 [16, 256, 1024], P(('grp', 'ang'), 'slab'), parts along dimension 0
- shift_slope: float32 [16], P(('grp', 'ang')), parts along dimension 0
There are 2 independent parts, one for each index of `grp`. A program takes and returns all parts, laid end to end along the dimension named above; an argument that names none is the same for every part. Nothing has to cross between parts.
All inputs are finite; a program needn't handle non-finite values.
Results may differ from a plain program's by a relative error of at most 0.006.
Values may be sent and summed in bfloat16 or wider, within the bound.
A program may use at most 128 MiB of HBM per device.

v0:
```python
import math
import jax
import jax.numpy as jnp
from jax import lax
from jax.sharding import PartitionSpec as P

Y = 256
X = 1024
U = 1024
OFF = 8
ROUNDS = 2
step_size = 0.5


def move_down(products, tilt_table):
    base = jnp.zeros((products.shape[1] + OFF, U), jnp.float32)
    placed = jax.vmap(
        lambda block, shift_rows: lax.dynamic_update_slice(base, block, (shift_rows, jnp.int32(0)))
    )(products, tilt_table)
    return jnp.sum(placed, axis=0)


def backproject(extended, tilt_table, ray_weights, band_rows):
    slices_count = tilt_table.shape[1]
    running = jnp.zeros((slices_count * band_rows, X), jnp.float32)
    for angle_index in range(ray_weights.shape[0]):
        source = extended[angle_index]
        picked = jax.vmap(
            lambda shift_rows: lax.dynamic_slice(source, (shift_rows, jnp.int32(0)), (band_rows, U))
        )(tilt_table[angle_index])
        running = running + lax.dot_general(
            picked.reshape(slices_count * band_rows, U),
            ray_weights[angle_index],
            (((1,), (1,)), ((), ())),
            preferred_element_type=jnp.float32,
        )
    return running


def apply_update(current, running):
    partial_value = lax.optimization_barrier(running.reshape(current.shape).astype(jnp.bfloat16))
    partial_wide = partial_value.astype(jnp.float32)
    gradient = lax.psum(partial_wide, "ang")
    renewed = (current.astype(jnp.float32) - step_size * gradient).astype(jnp.bfloat16)
    return renewed


def per_device(volume, ray_weights, row_offsets, measured, shifts):
    angles_here = ray_weights.shape[0]
    band_rows = measured.shape[1]
    highest = lax.Precision.HIGHEST
    numbers = lax.iota(jnp.int32, U)
    turns = numbers[:, None] * numbers[None, :] % U
    radians = turns.astype(jnp.float32) * (2.0 * math.pi / U)
    cosine = jnp.cos(radians)
    sine = jnp.sin(radians)
    signed = jnp.where(numbers <= (U - 1) // 2, numbers, numbers - U)
    omega = signed.astype(jnp.float32) * (2.0 * math.pi / U)
    flat_rows = measured.reshape(angles_here * band_rows, U)
    real_part = jnp.dot(flat_rows, cosine, precision=highest).reshape(angles_here, band_rows, U)
    imag_part = -jnp.dot(flat_rows, sine, precision=highest).reshape(angles_here, band_rows, U)
    phase = omega[None, None, :] * shifts[:, None, None]
    turned_real = real_part * jnp.cos(phase) + imag_part * jnp.sin(phase)
    turned_imag = imag_part * jnp.cos(phase) - real_part * jnp.sin(phase)
    first_half = jnp.concatenate([turned_real, omega * turned_imag], axis=0).reshape(-1, U)
    second_half = jnp.concatenate([turned_imag, -omega * turned_real], axis=0).reshape(-1, U)
    inverse = (
        jnp.dot(first_half, cosine, precision=highest)
        - jnp.dot(second_half, sine, precision=highest)
    ) / U
    inverse = inverse.reshape(2, angles_here, band_rows, U)
    shifted = inverse[0]
    slope_field = inverse[1]
    projection = shifted
    residual = shifted
    current = volume
    slices_here = volume.shape[0]
    tilt_table = lax.dynamic_slice_in_dim(
        row_offsets, lax.axis_index("slab") * slices_here, slices_here, 1
    )
    for round_index in range(ROUNDS):
        flattened = current.reshape(slices_here * Y, X)
        partials = jnp.stack(
            [
                move_down(
                    jnp.dot(
                        flattened, ray_weights[angle_index], preferred_element_type=jnp.float32
                    ).reshape(slices_here, Y, U),
                    tilt_table[angle_index],
                )[:Y]
                for angle_index in range(angles_here)
            ]
        )
        projection = lax.psum_scatter(partials, "slab", scatter_dimension=1, tiled=True)
        residual = projection - shifted
        rounded = residual.astype(jnp.bfloat16)
        gathered = lax.all_gather(rounded, "slab", axis=1, tiled=True)
        extended = jnp.concatenate(
            [gathered, jnp.zeros((angles_here, OFF, U), jnp.bfloat16)], axis=1
        )
        running = backproject(extended, tilt_table, ray_weights, Y)
        current = apply_update(current, running)
    local_dot = jnp.sum(projection * slope_field, axis=(1, 2))
    shift_slope = lax.psum(local_dot, "slab") / math.sqrt(Y * U)
    return (current, residual, shift_slope)


def solution(mesh):
    in_specs = (
        P(("grp", "slab"), None, None),
        P("ang", None, None),
        P("ang", None),
        P(("grp", "ang"), "slab", None),
        P(("grp", "ang")),
    )
    out_specs = (P(("grp", "slab"), None, None), P(("grp", "ang"), "slab", None), P(("grp", "ang")))
    return jax.shard_map(
        per_device, mesh=mesh, in_specs=in_specs, out_specs=out_specs, check_vma=False
    )
```

profile of v0, /device:TPU:1, one launch (start us, length us, event | category | flops | bytes accessed | tf_op | source)
XLA Modules:
  0.0 434.2 jit_solution(13662559025870306911)
XLA Ops:
  7.3 4.6 %fusion.16 = f32[2,256,1024]{2,1,0:T(8,128)} fusion(bf16[2,256,1024]{2,1,0:T(8,128)(2,1)} %param.5, bf16[2,1024,1024]{2,1,0:T(8,128)(2,1)} %param.6), kind=kOutput, calls=%fused_computation.41 | convolution fusion | flops 1073741824 | bytes 5242880 | tf_op jit(solution)/shard_map/dot_general | solution.py:86
  16.4 23.4 %while.12 = (s32[]{:T(128)}, f32[2,264,1024]{2,1,0:T(8,128)}, s32[2,3]{1,0:T(2,128)S(1)}, f32[2,256,1024]{2,1,0:T(8,128)}, s32[]{:T(128)}, /*index=5*/s32[3]{0:T(128)S(1)}, s32[]{:T(128)}) while((s32[]{:T(128)}, f32[2,264,1024]{2,1,0:T(8,128)}, s32[2,3]{1,0:T(2,128)S(1)}, f32[2,256,1024]{2,1,0:T(8,128)}, s32[]{:T(128)}, /*index=5*/s32[3]{0:T(128)S(1)}, ...), condition=%wide.while_cond.4, body=%wide.while_body.4.sunk | while | flops 262163 | bytes 5243051 | solution.py:18
  19.6 3.6 dynamic-slice_select_fusion.8
  23.2 4.9 %dynamic-update-slice.32 = f32[2,264,1024]{2,1,0:T(8,128)} dynamic-update-slice(f32[2,264,1024]{2,1,0:T(8,128)} %get-tuple-element.455, f32[1,256,1024]{2,1,0:T(8,128)S(1)} %dynamic-slice_select_fusion.8, s32[]{:T(128)} %bitcast.154, s32[]{:T(128)} %bitcast.155, s32[]{:T(128)} %constant.18.clone.1..sunk) | dynamic-update-slice | bytes 2097156 | tf_op jit(solution)/shard_map/vmap(vmap())/scatter
  31.3 3.6 dynamic-slice_select_fusion.8
  34.9 4.9 %dynamic-update-slice.32 = f32[2,264,1024]{2,1,0:T(8,128)} dynamic-update-slice(f32[2,264,1024]{2,1,0:T(8,128)} %get-tuple-element.455, f32[1,256,1024]{2,1,0:T(8,128)S(1)} %dynamic-slice_select_fusion.8, s32[]{:T(128)} %bitcast.154, s32[]{:T(128)} %bitcast.155, s32[]{:T(128)} %constant.18.clone.1..sunk) | dynamic-update-slice | bytes 2097156 | tf_op jit(solution)/shard_map/vmap(vmap())/scatter
  41.5 23.9 %while.13 = (s32[]{:T(128)}, f32[2,264,1024]{2,1,0:T(8,128)}, s32[2,3]{1,0:T(2,128)S(1)}, f32[2,256,1024]{2,1,0:T(8,128)}, s32[]{:T(128)}, /*index=5*/s32[3]{0:T(128)S(1)}, s32[]{:T(128)}) while((s32[]{:T(128)}, f32[2,264,1024]{2,1,0:T(8,128)}, s32[2,3]{1,0:T(2,128)S(1)}, f32[2,256,1024]{2,1,0:T(8,128)}, s32[]{:T(128)}, /*index=5*/s32[3]{0:T(128)S(1)}, ...), condition=%wide.while_cond.5, body=%wide.while_body.5.sunk | while | flops 262163 | bytes 5243051 | solution.py:18
  44.9 3.7 dynamic-slice_select_fusion.9
  48.6 5.0 %dynamic-update-slice.33 = f32[2,264,1024]{2,1,0:T(8,128)} dynamic-update-slice(f32[2,264,1024]{2,1,0:T(8,128)} %get-tuple-element.434, f32[1,256,1024]{2,1,0:T(8,128)S(1)} %dynamic-slice_select_fusion.9, s32[]{:T(128)} %bitcast.159, s32[]{:T(128)} %bitcast.160, s32[]{:T(128)} %constant.18.clone.1..sunk.1) | dynamic-update-slice | bytes 2097156 | tf_op jit(solution)/shard_map/vmap(vmap())/scatter
  57.0 3.7 dynamic-slice_select_fusion.9
  60.7 4.8 %dynamic-update-slice.33 = f32[2,264,1024]{2,1,0:T(8,128)} dynamic-update-slice(f32[2,264,1024]{2,1,0:T(8,128)} %get-tuple-element.434, f32[1,256,1024]{2,1,0:T(8,128)S(1)} %dynamic-slice_select_fusion.9, s32[]{:T(128)} %bitcast.159, s32[]{:T(128)} %bitcast.160, s32[]{:T(128)} %constant.18.clone.1..sunk.1) | dynamic-update-slice | bytes 2097156 | tf_op jit(solution)/shard_map/vmap(vmap())/scatter
  73.6 18.6 %fusion.26 = f32[1024,128]{0,1:T(8,128)S(1)} fusion(f32[128,1024]{1,0:T(8,128)S(1)} %bitcast.174), kind=kOutput, calls=%fused_computation.54 | convolution fusion | flops 1625292800 | bytes 1048576 | tf_op jit(solution)/shard_map/dot_general | solution.py:60
  92.2 18.7 %fusion.50 = f32[1024,128]{0,1:T(8,128)S(1)} fusion(f32[128,1024]{1,0:T(8,128)S(1)} %bitcast.175), kind=kOutput, calls=%fused_computation.67 | convolution fusion | flops 1625423872 | bytes 1048576 | tf_op jit(solution)/shard_map/dot_general | solution.py:61
  111.3 20.2 %fusion.24 = f32[256,1024]{1,0:T(8,128)S(1)} fusion(f32[256,1024]{1,0:T(8,128)S(1)} %bitcast.185), kind=kOutput, calls=%fused_computation.53 | convolution fusion | flops 3235905536 | bytes 2097152 | tf_op jit(solution)/shard_map/dot_general | solution.py:68
  131.5 20.1 %fusion.47 = f32[256,1024]{1,0:T(8,128)S(1)} fusion(f32[256,1024]{1,0:T(8,128)S(1)} %fusion.24, f32[256,1024]{1,0:T(8,128)S(1)} %bitcast.184), kind=kOutput, calls=%fused_computation.66 | convolution fusion | flops 3236429824 | bytes 3145728 | tf_op jit(solution)/shard_map/dot_general | solution.py:69
  153.8 29.5 %all-gather.3.cloned.1.call-done = bf16[2,256,1024]{2,1,0:T(8,128)(2,1)} async-done(((bf16[2,64,1024]{2,1,0:T(8,128)(2,1)}), bf16[2,256,1024]{2,1,0:T(8,128)(2,1)}) %all-gather.3.cloned.1.call-update) | async-done | bytes 1048592 | tf_op jit(solution)/shard_map/all_gather | solution.py:97
  185.3 4.2 fusion.10
  190.1 4.5 %add_convert_fusion.1 = bf16[512,1024]{1,0:T(8,128)(2,1)} fusion(f32[512,1024]{1,0:T(8,128)} %fusion.10, bf16[512,1024]{1,0:T(8,128)(2,1)S(1)} %bitcast.182, bf16[2,1024,1024]{2,1,0:T(8,128)(2,1)} %param.6), kind=kOutput, calls=%fused_computation.50 | convolution fusion | flops 1074790400 | bytes 6291456 | tf_op jit(solution)/shard_map/dot_general | solution.py:31
  194.6 42.1 %all-reduce.6 = f32[2,256,1024]{2,1,0:T(8,128)S(1)} all-reduce(bf16[2,256,1024]{2,1,0:T(8,128)(2,1)} %bitcast.178), channel_id=1, replica_groups=mesh['grp'=2,'slab'=4,'ang'=4] {'ang'}, use_global_device_ids=true, to_apply=%region_5.6 | all-reduce | flops 524288 | bytes 3145728 | tf_op jit(solution)/shard_map/psum | solution.py:43
  245.9 23.4 %while.14 = (s32[]{:T(128)}, f32[2,264,1024]{2,1,0:T(8,128)}, s32[2,3]{1,0:T(2,128)S(1)}, f32[2,256,1024]{2,1,0:T(8,128)}, s32[]{:T(128)}, /*index=5*/s32[3]{0:T(128)S(1)}, s32[]{:T(128)}) while((s32[]{:T(128)}, f32[2,264,1024]{2,1,0:T(8,128)}, s32[2,3]{1,0:T(2,128)S(1)}, f32[2,256,1024]{2,1,0:T(8,128)}, s32[]{:T(128)}, /*index=5*/s32[3]{0:T(128)S(1)}, ...), condition=%wide.while_cond.6, body=%wide.while_body.6.sunk | while | flops 262163 | bytes 5243051 | solution.py:18
  252.7 5.0 %dynamic-update-slice.34 = f32[2,264,1024]{2,1,0:T(8,128)} dynamic-update-slice(f32[2,264,1024]{2,1,0:T(8,128)} %get-tuple-element.527, f32[1,256,1024]{2,1,0:T(8,128)S(1)} %dynamic-slice_select_fusion.10, s32[]{:T(128)} %bitcast.164, s32[]{:T(128)} %bitcast.165, s32[]{:T(128)} %constant.18.clone.1..sunk.2) | dynamic-update-slice | bytes 2097156 | tf_op jit(solution)/shard_map/vmap(vmap())/scatter
  264.4 5.0 %dynamic-update-slice.34 = f32[2,264,1024]{2,1,0:T(8,128)} dynamic-update-slice(f32[2,264,1024]{2,1,0:T(8,128)} %get-tuple-element.527, f32[1,256,1024]{2,1,0:T(8,128)S(1)} %dynamic-slice_select_fusion.10, s32[]{:T(128)} %bitcast.164, s32[]{:T(128)} %bitcast.165, s32[]{:T(128)} %constant.18.clone.1..sunk.2) | dynamic-update-slice | bytes 2097156 | tf_op jit(solution)/shard_map/vmap(vmap())/scatter
  273.0 23.3 %while.15 = (s32[]{:T(128)}, f32[2,264,1024]{2,1,0:T(8,128)}, s32[2,3]{1,0:T(2,128)S(1)}, f32[2,256,1024]{2,1,0:T(8,128)}, s32[]{:T(128)}, /*index=5*/s32[3]{0:T(128)S(1)}, s32[]{:T(128)}) while((s32[]{:T(128)}, f32[2,264,1024]{2,1,0:T(8,128)}, s32[2,3]{1,0:T(2,128)S(1)}, f32[2,256,1024]{2,1,0:T(8,128)}, s32[]{:T(128)}, /*index=5*/s32[3]{0:T(128)S(1)}, ...), condition=%wide.while_cond.7, body=%wide.while_body.7.sunk | while | flops 262163 | bytes 5243051 | solution.py:18
  276.2 3.6 dynamic-slice_select_fusion.11
  279.8 5.0 %dynamic-update-slice.35 = f32[2,264,1024]{2,1,0:T(8,128)} dynamic-update-slice(f32[2,264,1024]{2,1,0:T(8,128)} %get-tuple-element.506, f32[1,256,1024]{2,1,0:T(8,128)S(1)} %dynamic-slice_select_fusion.11, s32[]{:T(128)} %bitcast.169, s32[]{:T(128)} %bitcast.170, s32[]{:T(128)} %constant.18.clone.1..sunk.3) | dynamic-update-slice | bytes 2097156 | tf_op jit(solution)/shard_map/vmap(vmap())/scatter
  291.5 4.7 %dynamic-update-slice.35 = f32[2,264,1024]{2,1,0:T(8,128)} dynamic-update-slice(f32[2,264,1024]{2,1,0:T(8,128)} %get-tuple-element.506, f32[1,256,1024]{2,1,0:T(8,128)S(1)} %dynamic-slice_select_fusion.11, s32[]{:T(128)} %bitcast.169, s32[]{:T(128)} %bitcast.170, s32[]{:T(128)} %constant.18.clone.1..sunk.3) | dynamic-update-slice | bytes 2097156 | tf_op jit(solution)/shard_map/vmap(vmap())/scatter
  299.9 42.4 %reduce-scatter.5.cloned.1.call-done = f32[2,64,1024]{2,1,0:T(8,128)} async-done(((f32[2,256,1024]{2,1,0:T(8,128)}), f32[2,64,1024]{2,1,0:T(8,128)}) %reduce-scatter.5.cloned.1.call-update) | async-done | bytes 524304 | tf_op jit(solution)/shard_map/reduce_scatter | solution.py:94
  344.4 8.7 %psum.23 = f32[2]{0:T(128)S(1)} all-reduce(f32[2]{0:T(128)S(1)} %get-tuple-element.189), channel_id=1, replica_groups=mesh['grp'=2,'slab'=4,'ang'=4] {'slab'}, use_global_device_ids=true, to_apply=%region_13.14 | all-reduce | flops 2 | bytes 16 | tf_op jit(solution)/shard_map/psum | solution.py:104
  353.6 18.1 %all-gather.5.cloned.1.call-done = bf16[2,256,1024]{2,1,0:T(8,128)(2,1)} async-done(((bf16[2,64,1024]{2,1,0:T(8,128)(2,1)}), bf16[2,256,1024]{2,1,0:T(8,128)(2,1)}) %all-gather.5.cloned.1.call-update) | async-done | bytes 1048592 | tf_op jit(solution)/shard_map/all_gather | solution.py:97
  373.5 4.2 fusion.12
  378.2 4.5 %add_convert_fusion = bf16[512,1024]{1,0:T(8,128)(2,1)} fusion(f32[512,1024]{1,0:T(8,128)} %fusion.12, bf16[512,1024]{1,0:T(8,128)(2,1)S(1)} %bitcast.180, bf16[2,1024,1024]{2,1,0:T(8,128)(2,1)} %param.6), kind=kOutput, calls=%fused_computation.48 | convolution fusion | flops 1074790400 | bytes 6291456 | tf_op jit(solution)/shard_map/dot_general | solution.py:31
  382.7 42.2 %all-reduce.7 = f32[2,256,1024]{2,1,0:T(8,128)S(1)} all-reduce(bf16[2,256,1024]{2,1,0:T(8,128)(2,1)} %bitcast.179), channel_id=1, replica_groups=mesh['grp'=2,'slab'=4,'ang'=4] {'ang'}, use_global_device_ids=true, to_apply=%region_11.12 | all-reduce | flops 524288 | bytes 3145728 | tf_op jit(solution)/shard_map/psum | solution.py:43
  (122 shorter events, 81.6 us)
Async XLA Ops:
  7.2 66.5 %copy-start = (f32[2,64,1024]{2,1,0:T(8,128)S(1)}, f32[2,64,1024]{2,1,0:T(8,128)}, u32[]{:S(2)}) copy-start(f32[2,64,1024]{2,1,0:T(8,128)} %param.8) | copy-start | bytes 1572868
  7.2 144.5 %reduce-scatter.3.cloned.1.call-start = ((), (), s32[]{:S(2)}) async-start(), calls=%async_computation.2 | async-start | bytes 2621440 | tf_op jit(solution)/shard_map/reduce_scatter | solution.py:94
  7.2 4.7 %copy-start.4 = (bf16[2,256,1024]{2,1,0:T(8,128)(2,1)S(1)}, bf16[2,256,1024]{2,1,0:T(8,128)(2,1)}, u32[]{:S(2)}) copy-start(bf16[2,256,1024]{2,1,0:T(8,128)(2,1)} %param.5) | copy-start | bytes 3145732
  7.2 4.7 %copy-start.9 = (bf16[2,1024,1024]{2,1,0:T(8,128)(2,1)S(1)}, bf16[2,1024,1024]{2,1,0:T(8,128)(2,1)}, u32[]{:S(2)}) copy-start(bf16[2,1024,1024]{2,1,0:T(8,128)(2,1)} %param.6) | copy-start | bytes 12582916
  11.9 2.6 copy-start.6
  11.9 2.7 copy-start.7
  14.5 1.9 copy-start.5
  65.4 3.0 copy-start.2
  71.4 2.0 copy-start.8
  72.9 110.4 %all-gather.3.cloned.1.call-start = ((), (), s32[]{:S(2)}) async-start(), calls=%async_computation.3 | async-start | bytes 1310720 | tf_op jit(solution)/shard_map/all_gather | solution.py:97
  153.6 188.7 %reduce-scatter.5.cloned.1.call-start = ((), (), s32[]{:S(2)}) async-start(), calls=%async_computation.4 | async-start | bytes 2621440 | tf_op jit(solution)/shard_map/reduce_scatter | solution.py:94
  236.6 2.5 copy-start.10
  239.1 2.6 copy-start.3
  299.8 71.8 %all-gather.5.cloned.1.call-start = ((), (), s32[]{:S(2)}) async-start(), calls=%async_computation.5 | async-start | bytes 1310720 | tf_op jit(solution)/shard_map/all_gather | solution.py:97
  382.7 44.7 %copy-start.1 = (f32[2,64,1024]{2,1,0:T(8,128)S(1)}, f32[2,64,1024]{2,1,0:T(8,128)}, u32[]{:S(2)}) copy-start(f32[2,64,1024]{2,1,0:T(8,128)} %param.8) | copy-start | bytes 1572868
Sparse Core Ops, SparseCore 0:
  73.0 45.3 reduce-scatter.2
  153.7 29.5 all-gather.2
  299.9 42.2 reduce-scatter.4
  344.5 27.0 all-gather.4
where the time goes:
time: 440 us; the launch traced here: 434 us
  matrix products  107 us (24%)
  blocking collectives  92.9 us (21%)
  waiting for transfers between devices  90 us (20%)
  other arithmetic  70.2 us (16%)
  local copies, waits for them, and re-layouts  58.4 us (13%)
  between operations  14.3 us (3%)
    psum x2, blocking collectives, apply_update(): gradient = lax.psum(partial_wide, 'ang')  84.2 us
    scatter x16, other arithmetic  49.8 us
    all_gather x2, waiting for transfers between devices, per_device(): gathered = lax.all_gather(rounded, 'slab', axis=1, tiled=True)  47.5 us
    scatter x24, local copies, waits for them, and re-layouts  44.2 us
    reduce_scatter x2, waiting for transfers between devices, per_device(): lax.psum_scatter(partials, 'slab', scatter_dimension=1, tiled=True)  42.4 us
    dot_general x1, matrix products, per_device(): jnp.dot(first_half, cosine, precision=highest)  20.2 us
    dot_general x1, matrix products, per_device(): jnp.dot(second_half, sine, precision=highest)  20.1 us
    dot_general x1, matrix products, per_device(): jnp.dot(flat_rows, sine, precision=highest)  18.7 us
  transfers between devices with their start and end apart: 4, of which 3 were waited for; matrix products, arithmetic and copies ran while one was open for 18% of the time, Pallas kernels for 0%

commit v1 on v0

--- a/solution.py
+++ b/solution.py
@@ -40,7 +40,7 @@
 def apply_update(current, running):
     partial_value = lax.optimization_barrier(running.reshape(current.shape).astype(jnp.bfloat16))
     partial_wide = partial_value.astype(jnp.float32)
-    gradient = lax.psum(partial_wide, "ang")
+    gradient = jnp.sum(lax.all_gather(partial_wide, "ang"), axis=0)
     renewed = (current.astype(jnp.float32) - step_size * gradient).astype(jnp.bfloat16)
     return renewed
 

time: 440 us -> 485 us (1.10)
  waiting for transfers between devices: 90 us -> 208 us
  blocking collectives: 92.9 us -> 8.5 us
  other arithmetic: 70.2 us -> 82.2 us
    all_gather x0 -> x2, waiting for transfers between devices: none -> 108 us  [apply_update(): gradient = jnp.sum(lax.all_gather(partial_wide, 'ang'), axis=0)]
    psum x2 -> x0, blocking collectives: 84.2 us -> none  [apply_update(): gradient = lax.psum(partial_wide, 'ang')]
    reduce_sum x0 -> x2, other arithmetic: none -> 9.16 us  [apply_update(): gradient = jnp.sum(lax.all_gather(partial_wide, 'ang'), axis=0)]
    all_gather x2, waiting for transfers between devices: 47.5 us -> 56.7 us  [per_device(): gathered = lax.all_gather(rounded, 'slab', axis=1, tiled=True)]
  transfers between devices with their start and end apart: 4 -> 6, of which waited for: 3 -> 5; matrix products, arithmetic and copies ran while one was open for 18% -> 16% of each run, Pallas kernels for 0% -> 0%
where the time goes in v1:
time: 485 us; the launch traced here: 479 us
  waiting for transfers between devices  208 us (43%)
  matrix products  105 us (22%)
  other arithmetic  82.2 us (17%)
  local copies, waits for them, and re-layouts  58.6 us (12%)
  between operations  14.7 us (3%)
  blocking collectives  8.5 us (2%)
    all_gather x2, waiting for transfers between devices, apply_update(): gradient = jnp.sum(lax.all_gather(partial_wide, 'ang'), axis=0)  108 us
    all_gather x2, waiting for transfers between devices, per_device(): gathered = lax.all_gather(rounded, 'slab', axis=1, tiled=True)  56.7 us
    scatter x16, other arithmetic  49.3 us
    scatter x24, local copies, waits for them, and re-layouts  44.4 us
    reduce_scatter x2, waiting for transfers between devices, per_device(): lax.psum_scatter(partials, 'slab', scatter_dimension=1, tiled=True)  43.2 us
    dot_general x1, matrix products, per_device(): jnp.dot(first_half, cosine, precision=highest)  20.2 us
    dot_general x1, matrix products, per_device(): jnp.dot(second_half, sine, precision=highest)  20.1 us
    dot_general x1, matrix products, per_device(): jnp.dot(flat_rows, sine, precision=highest)  18.6 us
  transfers between devices with their start and end apart: 6, of which 5 were waited for; matrix products, arithmetic and copies ran while one was open for 16% of the time, Pallas kernels for 0%

profile of v1, /device:TPU:1, one launch (start us, length us, event | category | flops | bytes accessed | tf_op | source)
XLA Modules:
  0.0 478.8 jit_solution(5865099235029505596)
XLA Ops:
  7.3 4.6 fusion.16
  16.4 24.1 %while.12 = (s32[]{:T(128)}, f32[2,264,1024]{2,1,0:T(8,128)}, s32[2,3]{1,0:T(2,128)S(1)}, f32[2,256,1024]{2,1,0:T(8,128)}, s32[]{:T(128)}, /*index=5*/s32[3]{0:T(128)S(1)}, s32[]{:T(128)}) while((s32[]{:T(128)}, f32[2,264,1024]{2,1,0:T(8,128)}, s32[2,3]{1,0:T(2,128)S(1)}, f32[2,256,1024]{2,1,0:T(8,128)}, s32[]{:T(128)}, /*index=5*/s32[3]{0:T(128)S(1)}, ...), condition=%wide.while_cond.4, body=%wide.while_body.4.sunk | while | flops 262163 | bytes 5243051 | solution.py:18
  19.7 3.7 dynamic-slice_select_fusion.8
  23.4 5.1 %dynamic-update-slice.32 = f32[2,264,1024]{2,1,0:T(8,128)} dynamic-update-slice(f32[2,264,1024]{2,1,0:T(8,128)} %get-tuple-element.487, f32[1,256,1024]{2,1,0:T(8,128)S(1)} %dynamic-slice_select_fusion.8, s32[]{:T(128)} %bitcast.156, s32[]{:T(128)} %bitcast.157, s32[]{:T(128)} %constant.18.clone.1..sunk) | dynamic-update-slice | bytes 2097156 | tf_op jit(solution)/shard_map/vmap(vmap())/scatter
  31.8 3.7 dynamic-slice_select_fusion.8
  35.5 5.1 %dynamic-update-slice.32 = f32[2,264,1024]{2,1,0:T(8,128)} dynamic-update-slice(f32[2,264,1024]{2,1,0:T(8,128)} %get-tuple-element.487, f32[1,256,1024]{2,1,0:T(8,128)S(1)} %dynamic-slice_select_fusion.8, s32[]{:T(128)} %bitcast.156, s32[]{:T(128)} %bitcast.157, s32[]{:T(128)} %constant.18.clone.1..sunk) | dynamic-update-slice | bytes 2097156 | tf_op jit(solution)/shard_map/vmap(vmap())/scatter
  42.3 23.5 %while.13 = (s32[]{:T(128)}, f32[2,264,1024]{2,1,0:T(8,128)}, s32[2,3]{1,0:T(2,128)S(1)}, f32[2,256,1024]{2,1,0:T(8,128)}, s32[]{:T(128)}, /*index=5*/s32[3]{0:T(128)S(1)}, s32[]{:T(128)}) while((s32[]{:T(128)}, f32[2,264,1024]{2,1,0:T(8,128)}, s32[2,3]{1,0:T(2,128)S(1)}, f32[2,256,1024]{2,1,0:T(8,128)}, s32[]{:T(128)}, /*index=5*/s32[3]{0:T(128)S(1)}, ...), condition=%wide.while_cond.5, body=%wide.while_body.5.sunk | while | flops 262163 | bytes 5243051 | solution.py:18
  45.5 3.6 dynamic-slice_select_fusion.9
  49.2 5.0 %dynamic-update-slice.33 = f32[2,264,1024]{2,1,0:T(8,128)} dynamic-update-slice(f32[2,264,1024]{2,1,0:T(8,128)} %get-tuple-element.466, f32[1,256,1024]{2,1,0:T(8,128)S(1)} %dynamic-slice_select_fusion.9, s32[]{:T(128)} %bitcast.161, s32[]{:T(128)} %bitcast.162, s32[]{:T(128)} %constant.18.clone.1..sunk.1) | dynamic-update-slice | bytes 2097156 | tf_op jit(solution)/shard_map/vmap(vmap())/scatter
  57.4 3.6 dynamic-slice_select_fusion.9
  61.0 4.8 dynamic-update-slice.33
  74.0 18.6 %fusion.26 = f32[1024,128]{0,1:T(8,128)S(1)} fusion(f32[128,1024]{1,0:T(8,128)S(1)} %bitcast.176), kind=kOutput, calls=%fused_computation.54 | convolution fusion | flops 1625292800 | bytes 1048576 | tf_op jit(solution)/shard_map/dot_general | solution.py:60
  92.6 18.6 %fusion.50 = f32[1024,128]{0,1:T(8,128)S(1)} fusion(f32[128,1024]{1,0:T(8,128)S(1)} %bitcast.177), kind=kOutput, calls=%fused_computation.67 | convolution fusion | flops 1625423872 | bytes 1048576 | tf_op jit(solution)/shard_map/dot_general | solution.py:61
  111.7 20.2 %fusion.24 = f32[256,1024]{1,0:T(8,128)S(1)} fusion(f32[256,1024]{1,0:T(8,128)S(1)} %bitcast.189), kind=kOutput, calls=%fused_computation.53 | convolution fusion | flops 3235905536 | bytes 2097152 | tf_op jit(solution)/shard_map/dot_general | solution.py:68
  131.8 20.1 %fusion.47 = f32[256,1024]{1,0:T(8,128)S(1)} fusion(f32[256,1024]{1,0:T(8,128)S(1)} %fusion.24, f32[256,1024]{1,0:T(8,128)S(1)} %bitcast.188), kind=kOutput, calls=%fused_computation.66 | convolution fusion | flops 3236429824 | bytes 3145728 | tf_op jit(solution)/shard_map/dot_general | solution.py:69
  154.1 29.5 %all-gather.7.cloned.1.call-done = bf16[2,256,1024]{2,1,0:T(8,128)(2,1)} async-done(((bf16[2,64,1024]{2,1,0:T(8,128)(2,1)}), bf16[2,256,1024]{2,1,0:T(8,128)(2,1)}) %all-gather.7.cloned.1.call-update) | async-done | bytes 1048592 | tf_op jit(solution)/shard_map/all_gather | solution.py:97
  185.7 4.2 fusion.10
  190.5 3.5 add_convert_fusion.1
  195.7 58.6 %all-gather.11.cloned.1.call-done = f32[8,256,1024]{2,1,0:T(8,128)} async-done(((f32[2,256,1024]{2,1,0:T(8,128)}), f32[8,256,1024]{2,1,0:T(8,128)}) %all-gather.11.cloned.1.call-update) | async-done | bytes 8388624 | tf_op jit(solution)/shard_map/all_gather | solution.py:43
  254.3 4.6 reduce_sum.65
  268.2 23.2 %while.14 = (s32[]{:T(128)}, f32[2,264,1024]{2,1,0:T(8,128)}, s32[2,3]{1,0:T(2,128)S(1)}, f32[2,256,1024]{2,1,0:T(8,128)}, s32[]{:T(128)}, /*index=5*/s32[3]{0:T(128)S(1)}, s32[]{:T(128)}) while((s32[]{:T(128)}, f32[2,264,1024]{2,1,0:T(8,128)}, s32[2,3]{1,0:T(2,128)S(1)}, f32[2,256,1024]{2,1,0:T(8,128)}, s32[]{:T(128)}, /*index=5*/s32[3]{0:T(128)S(1)}, ...), condition=%wide.while_cond.6, body=%wide.while_body.6.sunk | while | flops 262163 | bytes 5243051 | solution.py:18
  274.9 4.9 %dynamic-update-slice.34 = f32[2,264,1024]{2,1,0:T(8,128)} dynamic-update-slice(f32[2,264,1024]{2,1,0:T(8,128)} %get-tuple-element.559, f32[1,256,1024]{2,1,0:T(8,128)S(1)} %dynamic-slice_select_fusion.10, s32[]{:T(128)} %bitcast.166, s32[]{:T(128)} %bitcast.167, s32[]{:T(128)} %constant.18.clone.1..sunk.2) | dynamic-update-slice | bytes 2097156 | tf_op jit(solution)/shard_map/vmap(vmap())/scatter
  286.5 4.9 %dynamic-update-slice.34 = f32[2,264,1024]{2,1,0:T(8,128)} dynamic-update-slice(f32[2,264,1024]{2,1,0:T(8,128)} %get-tuple-element.559, f32[1,256,1024]{2,1,0:T(8,128)S(1)} %dynamic-slice_select_fusion.10, s32[]{:T(128)} %bitcast.166, s32[]{:T(128)} %bitcast.167, s32[]{:T(128)} %constant.18.clone.1..sunk.2) | dynamic-update-slice | bytes 2097156 | tf_op jit(solution)/shard_map/vmap(vmap())/scatter
  295.0 22.9 %while.15 = (s32[]{:T(128)}, f32[2,264,1024]{2,1,0:T(8,128)}, s32[2,3]{1,0:T(2,128)S(1)}, f32[2,256,1024]{2,1,0:T(8,128)}, s32[]{:T(128)}, /*index=5*/s32[3]{0:T(128)S(1)}, s32[]{:T(128)}) while((s32[]{:T(128)}, f32[2,264,1024]{2,1,0:T(8,128)}, s32[2,3]{1,0:T(2,128)S(1)}, f32[2,256,1024]{2,1,0:T(8,128)}, s32[]{:T(128)}, /*index=5*/s32[3]{0:T(128)S(1)}, ...), condition=%wide.while_cond.7, body=%wide.while_body.7.sunk | while | flops 262163 | bytes 5243051 | solution.py:18
  301.7 4.8 %dynamic-update-slice.35 = f32[2,264,1024]{2,1,0:T(8,128)} dynamic-update-slice(f32[2,264,1024]{2,1,0:T(8,128)} %get-tuple-element.538, f32[1,256,1024]{2,1,0:T(8,128)S(1)} %dynamic-slice_select_fusion.11, s32[]{:T(128)} %bitcast.171, s32[]{:T(128)} %bitcast.172, s32[]{:T(128)} %constant.18.clone.1..sunk.3) | dynamic-update-slice | bytes 2097156 | tf_op jit(solution)/shard_map/vmap(vmap())/scatter
  313.3 4.6 dynamic-update-slice.35
  321.5 43.2 %reduce-scatter.5.cloned.1.call-done = f32[2,64,1024]{2,1,0:T(8,128)} async-done(((f32[2,256,1024]{2,1,0:T(8,128)}), f32[2,64,1024]{2,1,0:T(8,128)}) %reduce-scatter.5.cloned.1.call-update) | async-done | bytes 524304 | tf_op jit(solution)/shard_map/reduce_scatter | solution.py:94
  366.9 27.2 %all-gather.9.cloned.1.call-done = bf16[2,256,1024]{2,1,0:T(8,128)(2,1)} async-done(((bf16[2,64,1024]{2,1,0:T(8,128)(2,1)}), bf16[2,256,1024]{2,1,0:T(8,128)(2,1)}) %all-gather.9.cloned.1.call-update) | async-done | bytes 1048592 | tf_op jit(solution)/shard_map/all_gather | solution.py:97
  395.9 4.2 fusion.12
  405.8 8.5 %psum.7 = f32[2]{0:T(128)S(1)} all-reduce(f32[2]{0:T(128)S(1)} %get-tuple-element.221), channel_id=1, replica_groups=mesh['grp'=2,'slab'=4,'ang'=4] {'slab'}, use_global_device_ids=true, to_apply=%region_13.14 | all-reduce | flops 2 | bytes 16 | tf_op jit(solution)/shard_map/psum | solution.py:104
  414.9 49.7 %all-gather.13.cloned.1.call-done = f32[8,256,1024]{2,1,0:T(8,128)} async-done(((f32[2,256,1024]{2,1,0:T(8,128)}), f32[8,256,1024]{2,1,0:T(8,128)}) %all-gather.13.cloned.1.call-update) | async-done | bytes 8388624 | tf_op jit(solution)/shard_map/all_gather | solution.py:43
  464.5 4.6 reduce_sum.68
  (130 shorter events, 91.8 us)
Async XLA Ops:
  7.2 66.8 %copy-start = (f32[2,64,1024]{2,1,0:T(8,128)S(1)}, f32[2,64,1024]{2,1,0:T(8,128)}, u32[]{:S(2)}) copy-start(f32[2,64,1024]{2,1,0:T(8,128)} %param.8) | copy-start | bytes 1572868
  7.2 144.9 %reduce-scatter.3.cloned.1.call-start = ((), (), s32[]{:S(2)}) async-start(), calls=%async_computation.2 | async-start | bytes 2621440 | tf_op jit(solution)/shard_map/reduce_scatter | solution.py:94
  7.2 4.7 copy-start.4
  7.2 4.7 copy-start.9
  11.9 2.7 copy-start.6
  11.9 2.7 copy-start.7
  14.6 1.9 copy-start.5
  65.8 3.0 copy-start.2
  71.7 2.0 copy-start.8
  73.2 110.4 %all-gather.7.cloned.1.call-start = ((), (), s32[]{:S(2)}) async-start(), calls=%async_computation.3 | async-start | bytes 1310720 | tf_op jit(solution)/shard_map/all_gather | solution.py:97
  153.9 100.4 %all-gather.11.cloned.1.call-start = ((), (), s32[]{:S(2)}) async-start(), calls=%async_computation.6 | async-start | bytes 10485760 | tf_op jit(solution)/shard_map/all_gather | solution.py:43
  195.6 169.1 %reduce-scatter.5.cloned.1.call-start = ((), (), s32[]{:S(2)}) async-start(), calls=%async_computation.4 | async-start | bytes 2621440 | tf_op jit(solution)/shard_map/reduce_scatter | solution.py:94
  258.9 2.5 copy-start.10
  261.4 2.6 copy-start.3
  321.5 72.6 %all-gather.9.cloned.1.call-start = ((), (), s32[]{:S(2)}) async-start(), calls=%async_computation.5 | async-start | bytes 1310720 | tf_op jit(solution)/shard_map/all_gather | solution.py:97
  366.8 97.7 %all-gather.13.cloned.1.call-start = ((), (), s32[]{:S(2)}) async-start(), calls=%async_computation.7 | async-start | bytes 10485760 | tf_op jit(solution)/shard_map/all_gather | solution.py:43
  464.5 7.2 %copy-start.1 = (f32[2,64,1024]{2,1,0:T(8,128)S(1)}, f32[2,64,1024]{2,1,0:T(8,128)}, u32[]{:S(2)}) copy-start(f32[2,64,1024]{2,1,0:T(8,128)} %param.8) | copy-start | bytes 1572868
Sparse Core Ops, SparseCore 0:
  73.3 45.3 reduce-scatter.2
  154.0 29.5 all-gather.6
  195.7 58.5 all-gather.10
  321.6 43.0 reduce-scatter.4
  366.9 27.0 all-gather.8
  406.0 58.5 all-gather.12
